TPU v7x, 32 devices: a whole 2x2x4 slice. The times are simulated.
32 devices in a mesh: ctx: 8 (over y, x, core), tp: 4 (over z).
Axes of the slice: x: 2, y: 2, z: 4, core: 2. Of those that a mesh axis runs over, the one named last changes fastest.
Arguments:
- queries: bfloat16 [1024, 16384], P('ctx', 'tp'), may hold values from -110 to 110
- key_value_cache: bfloat16 [2, 5120, 1024], P(None, 'ctx', 'tp'), may hold values from -9 to 9
- cache_lengths: int32 [8], P('ctx'), may hold values from 64 to 512, as said below
- token_order: int32 [1024], P('ctx'), may hold values from 0 to 1023, each once
- out_weight: bfloat16 [16384, 16384], P('tp', 'ctx'), may hold values from -0.046875 to 0.046875
Outputs:
- output: bfloat16 [1024, 16384], P('tp', 'ctx')
Inputs may be any that keep to these rules, and one draw needn't show every extreme that they name: `cache_lengths`: one shard's cache is full in every draw. `token_order`: each number of 0 to 1023 stands once.
All inputs are finite; a program needn't handle non-finite values.
Results may differ from a plain program's by a relative error of at most 0.04.
Values may be sent and summed in bfloat16 or wider, within the bound.
A program may use at most 64 MiB of HBM per device.

v0:
```python
import math

import jax
import jax.numpy as jnp
from jax import lax
from jax.sharding import PartitionSpec as P

QUERY_HEADS = 128
KEY_VALUE_HEADS = 8
HEAD_SIZE = 128
TOKENS_PER_SHARD = 128
CACHE_DEV = 512
SHARD_ROWS = 640


masked_floor = -1e30
key_block = 512


def table_entry(table, position):
    return jnp.sum(jnp.where(jnp.arange(table.shape[0]) == position, table, 0))


def split_heads(block_slice):
    return block_slice.reshape(block_slice.shape[0], -1, QUERY_HEADS // KEY_VALUE_HEADS, HEAD_SIZE)


def fresh_state(grouped_heads, token_count):
    array_shape = (grouped_heads, QUERY_HEADS // KEY_VALUE_HEADS, token_count)
    return (
        jnp.full(array_shape, masked_floor, jnp.float32),
        jnp.zeros(array_shape, jnp.float32),
        jnp.zeros(array_shape + (HEAD_SIZE,), jnp.float32),
    )


def absorb(state, query_heads, key_matrix, value_matrix, allowed):
    running_max, running_total, weighted = state
    scores = jnp.einsum(
        "tkgd,nkd->kgtn", query_heads, key_matrix, preferred_element_type=jnp.float32
    ) * (1.0 / math.sqrt(HEAD_SIZE))
    scores = jnp.where(allowed[None, None], scores, -jnp.inf)
    new_max = jnp.maximum(running_max, jnp.max(scores, axis=-1))
    rescale = jnp.exp(running_max - new_max)
    raised = jnp.exp(scores - new_max[..., None])
    new_total = running_total * rescale + jnp.sum(raised, axis=-1)
    update = jnp.einsum(
        "kgtn,nkd->kgtd",
        raised.astype(jnp.bfloat16),
        value_matrix,
        preferred_element_type=jnp.float32,
    )
    return (new_max, new_total, weighted * rescale[..., None] + update)


def absorb_shard(state, query_heads, query_order, shard_rows, shard_index, length, order_all):
    grouped_heads = query_heads.shape[1]
    block_slice = min(key_block, CACHE_DEV)

    def cache_block(number_count, carry):
        begin = number_count * block_slice
        rows = lax.dynamic_slice_in_dim(shard_rows, begin, block_slice, 1)
        key_matrix = rows[0].reshape(block_slice, grouped_heads, HEAD_SIZE)
        value_matrix = rows[1].reshape(block_slice, grouped_heads, HEAD_SIZE)
        allowed = (begin + jnp.arange(block_slice) < length)[None, :]

        def taken(inner):
            return absorb(inner, query_heads, key_matrix, value_matrix, allowed)

        def skipped(inner):
            return inner

        return lax.cond(begin < length, taken, skipped, carry)

    state = lax.fori_loop(0, CACHE_DEV // block_slice, cache_block, state)
    fresh_rows = shard_rows[:, CACHE_DEV:]
    key_order = lax.dynamic_slice_in_dim(
        order_all, shard_index * TOKENS_PER_SHARD, TOKENS_PER_SHARD
    )
    allowed = key_order[None, :] <= query_order[:, None]
    fresh_keys = fresh_rows[0].reshape(TOKENS_PER_SHARD, grouped_heads, HEAD_SIZE)
    fresh_values = fresh_rows[1].reshape(TOKENS_PER_SHARD, grouped_heads, HEAD_SIZE)
    return absorb(state, query_heads, fresh_keys, fresh_values, allowed)


def body(queries, key_value_cache, cache_lengths, token_order, out_weight):
    order_all, lengths_all = (
        lax.all_gather(token_order, "ctx", axis=0, tiled=True),
        lax.all_gather(cache_lengths, "ctx", axis=0, tiled=True),
    )
    device = lax.axis_index("ctx")
    token_count = queries.shape[0]
    grouped_heads = key_value_cache.shape[2] // HEAD_SIZE
    own_order = lax.dynamic_slice_in_dim(order_all, device * TOKENS_PER_SHARD, TOKENS_PER_SHARD)
    query_heads = split_heads(queries)
    piece = lax.all_gather(key_value_cache, "ctx", axis=1, tiled=True)

    def one_shard(number_count, inner):
        rows = lax.dynamic_slice_in_dim(piece, number_count * SHARD_ROWS, SHARD_ROWS, 1)
        return absorb_shard(
            inner,
            query_heads,
            own_order,
            rows,
            number_count,
            table_entry(lengths_all, number_count),
            order_all,
        )

    running_max, total, combined = lax.fori_loop(
        0, piece.shape[1] // SHARD_ROWS, one_shard, fresh_state(grouped_heads, token_count)
    )
    attended = (
        jnp.transpose(combined / total[..., None], (2, 0, 1, 3))
        .reshape(token_count, -1)
        .astype(jnp.bfloat16)
    )
    terms = jnp.dot(
        lax.all_gather(attended, "ctx", axis=0, tiled=True),
        out_weight,
        preferred_element_type=jnp.float32,
    )
    return lax.psum_scatter(terms.astype(jnp.bfloat16), "tp", scatter_dimension=0, tiled=True)


def solution(mesh):
    placed = (P("ctx", "tp"), P(None, "ctx", "tp"), P("ctx"), P("ctx"), P("tp", "ctx"))
    return jax.shard_map(
        body, mesh=mesh, in_specs=placed, out_specs=P("tp", "ctx"), check_vma=False
    )
```

profile of v0, /device:TPU:0, one launch (start us, length us, event | category | flops | bytes accessed | tf_op | source)
XLA Modules:
  0.0 362.6 jit_solution(11289706846275653456)
XLA Ops:
  6.5 2.3 copy.24
  11.6 9.5 %all-reduce = s32[8]{0:T(128)S(1)} all-reduce(s32[8]{0:T(128)S(1)} %dynamic-update-slice), channel_id=1, replica_groups=mesh['ctx'=8,'tp'=4] {'ctx'}, use_global_device_ids=true, to_apply=%add | all-reduce | flops 8 | bytes 64
  22.5 8.3 %all-gather = s32[8,1,128]{2,1,0:T(1,128)S(1)} all-gather(s32[1,1,128]{2,1,0:T(1,128)S(1)} %bitcast.67), channel_id=1, replica_groups=mesh['ctx'=8,'tp'=4] {'ctx'}, dimensions={0}, use_global_device_ids=true | all-gather | bytes 4608 | tf_op jit(solution)/shard_map/all_gather | solution.py:88
  30.8 22.1 %all-gather.4.cloned.1.call-done = bf16[2,5120,256]{1,2,0:T(8,128)(2,1)} async-done(((bf16[2,640,256]{1,2,0:T(8,128)(2,1)}), bf16[2,5120,256]{1,2,0:T(8,128)(2,1)}) %all-gather.4.cloned.1.call-update) | async-done | bytes 5242896 | tf_op jit(solution)/shard_map/all_gather | solution.py:96
  52.9 143.1 %while.39 = (s32[]{:T(128)}, f32[2,16,128]{2,1,0:T(8,128)S(1)}, f32[2,16,128]{2,1,0:T(8,128)S(1)}, f32[2,16,128,128]{3,2,1,0:T(8,128)}, s32[8]{0:T(128)S(1)}, /*...) while((s32[]{:T(128)}, f32[2,16,128]{2,1,0:T(8,128)S(1)}, ...), condition=%wide.region_8.9_spmd.clone, body=%wide.region_0.8_spmd.clone.sunk | while | flops 1371578880 | bytes 50012628 | solution.py:110
  56.5 8.9 %conditional.3 = ((f32[2,16,128]{2,1,0:T(8,128)S(1)}, f32[2,16,128]{2,1,0:T(8,128)S(1)}, f32[2,16,128,128]{3,2,1,0:T(8,128)S(1)})) conditional(s32[]{:T(128)} %convert_element_type.47, (f32[2,16,128]{2,1,0:T(8,128)S(1)}, f32[2,16,128]{2,1,0:T(8,128)S(1)}, f32[2,16,128,128]{3,2,1,0:T(8,128)S(1)}) %tuple.64, (s32[]{:T(128)}, s32[512]{0:T(512)S(1)}, ...), branch_computations={%region_2.2_spmd, %region_3.5_spmd} | conditional | flops 1097867776 | bytes 32247844 | solution.py:73
  62.3 3.0 multiply_add_fusion
  74.5 8.9 %conditional.3 = ((f32[2,16,128]{2,1,0:T(8,128)S(1)}, f32[2,16,128]{2,1,0:T(8,128)S(1)}, f32[2,16,128,128]{3,2,1,0:T(8,128)S(1)})) conditional(s32[]{:T(128)} %convert_element_type.47, (f32[2,16,128]{2,1,0:T(8,128)S(1)}, f32[2,16,128]{2,1,0:T(8,128)S(1)}, f32[2,16,128,128]{3,2,1,0:T(8,128)S(1)}) %tuple.64, (s32[]{:T(128)}, s32[512]{0:T(512)S(1)}, ...), branch_computations={%region_2.2_spmd, %region_3.5_spmd} | conditional | flops 1097867776 | bytes 32247844 | solution.py:73
  80.4 3.0 multiply_add_fusion
  92.6 8.9 %conditional.3 = ((f32[2,16,128]{2,1,0:T(8,128)S(1)}, f32[2,16,128]{2,1,0:T(8,128)S(1)}, f32[2,16,128,128]{3,2,1,0:T(8,128)S(1)})) conditional(s32[]{:T(128)} %convert_element_type.47, (f32[2,16,128]{2,1,0:T(8,128)S(1)}, f32[2,16,128]{2,1,0:T(8,128)S(1)}, f32[2,16,128,128]{3,2,1,0:T(8,128)S(1)}) %tuple.64, (s32[]{:T(128)}, s32[512]{0:T(512)S(1)}, ...), branch_computations={%region_2.2_spmd, %region_3.5_spmd} | conditional | flops 1097867776 | bytes 32247844 | solution.py:73
  98.5 3.0 multiply_add_fusion
  110.7 8.9 %conditional.3 = ((f32[2,16,128]{2,1,0:T(8,128)S(1)}, f32[2,16,128]{2,1,0:T(8,128)S(1)}, f32[2,16,128,128]{3,2,1,0:T(8,128)S(1)})) conditional(s32[]{:T(128)} %convert_element_type.47, (f32[2,16,128]{2,1,0:T(8,128)S(1)}, f32[2,16,128]{2,1,0:T(8,128)S(1)}, f32[2,16,128,128]{3,2,1,0:T(8,128)S(1)}) %tuple.64, (s32[]{:T(128)}, s32[512]{0:T(512)S(1)}, ...), branch_computations={%region_2.2_spmd, %region_3.5_spmd} | conditional | flops 1097867776 | bytes 32247844 | solution.py:73
  116.6 3.0 multiply_add_fusion
  128.8 8.9 %conditional.3 = ((f32[2,16,128]{2,1,0:T(8,128)S(1)}, f32[2,16,128]{2,1,0:T(8,128)S(1)}, f32[2,16,128,128]{3,2,1,0:T(8,128)S(1)})) conditional(s32[]{:T(128)} %convert_element_type.47, (f32[2,16,128]{2,1,0:T(8,128)S(1)}, f32[2,16,128]{2,1,0:T(8,128)S(1)}, f32[2,16,128,128]{3,2,1,0:T(8,128)S(1)}) %tuple.64, (s32[]{:T(128)}, s32[512]{0:T(512)S(1)}, ...), branch_computations={%region_2.2_spmd, %region_3.5_spmd} | conditional | flops 1097867776 | bytes 32247844 | solution.py:73
  134.7 3.0 multiply_add_fusion
  146.9 8.9 %conditional.3 = ((f32[2,16,128]{2,1,0:T(8,128)S(1)}, f32[2,16,128]{2,1,0:T(8,128)S(1)}, f32[2,16,128,128]{3,2,1,0:T(8,128)S(1)})) conditional(s32[]{:T(128)} %convert_element_type.47, (f32[2,16,128]{2,1,0:T(8,128)S(1)}, f32[2,16,128]{2,1,0:T(8,128)S(1)}, f32[2,16,128,128]{3,2,1,0:T(8,128)S(1)}) %tuple.64, (s32[]{:T(128)}, s32[512]{0:T(512)S(1)}, ...), branch_computations={%region_2.2_spmd, %region_3.5_spmd} | conditional | flops 1097867776 | bytes 32247844 | solution.py:73
  152.8 3.0 multiply_add_fusion
  165.0 8.9 %conditional.3 = ((f32[2,16,128]{2,1,0:T(8,128)S(1)}, f32[2,16,128]{2,1,0:T(8,128)S(1)}, f32[2,16,128,128]{3,2,1,0:T(8,128)S(1)})) conditional(s32[]{:T(128)} %convert_element_type.47, (f32[2,16,128]{2,1,0:T(8,128)S(1)}, f32[2,16,128]{2,1,0:T(8,128)S(1)}, f32[2,16,128,128]{3,2,1,0:T(8,128)S(1)}) %tuple.64, (s32[]{:T(128)}, s32[512]{0:T(512)S(1)}, ...), branch_computations={%region_2.2_spmd, %region_3.5_spmd} | conditional | flops 1097867776 | bytes 32247844 | solution.py:73
  170.8 3.0 multiply_add_fusion
  183.1 8.9 %conditional.3 = ((f32[2,16,128]{2,1,0:T(8,128)S(1)}, f32[2,16,128]{2,1,0:T(8,128)S(1)}, f32[2,16,128,128]{3,2,1,0:T(8,128)S(1)})) conditional(s32[]{:T(128)} %convert_element_type.47, (f32[2,16,128]{2,1,0:T(8,128)S(1)}, f32[2,16,128]{2,1,0:T(8,128)S(1)}, f32[2,16,128,128]{3,2,1,0:T(8,128)S(1)}) %tuple.64, (s32[]{:T(128)}, s32[512]{0:T(512)S(1)}, ...), branch_computations={%region_2.2_spmd, %region_3.5_spmd} | conditional | flops 1097867776 | bytes 32247844 | solution.py:73
  188.9 3.0 multiply_add_fusion
  199.5 55.8 %all-gather.6.cloned.1.call-done = bf16[1024,4096]{0,1:T(8,128)(2,1)} async-done(((bf16[128,4096]{0,1:T(8,128)(2,1)}), bf16[1024,4096]{0,1:T(8,128)(2,1)}) %all-gather.6.cloned.1.call-update) | async-done | bytes 8388624 | tf_op jit(solution)/shard_map/all_gather | solution.py:119
  255.3 23.8 %convolution_convert_fusion = bf16[1024,2048]{1,0:T(8,128)(2,1)} fusion(bf16[1024,4096]{0,1:T(8,128)(2,1)} %all-gather.6.cloned.1.call-done, bf16[4096,2048]{1,0:T(8,128)(2,1)} %param.13), kind=kOutput, calls=%fused_computation.31 | convolution fusion | flops 17181966336 | bytes 29360128 | tf_op jit(solution)/shard_map/dot_general | solution.py:118
  279.1 77.0 %reduce-scatter.2.cloned.1.call-done = bf16[256,2048]{1,0:T(8,128)(2,1)} async-done(((bf16[1024,2048]{1,0:T(8,128)(2,1)}), bf16[256,2048]{1,0:T(8,128)(2,1)}) %reduce-scatter.2.cloned.1.call-update) | async-done | bytes 1048592 | tf_op jit(solution)/shard_map/reduce_scatter | solution.py:123
  (181 shorter events, 119.4 us)
Async XLA Ops:
  6.5 14.6 %copy-start = (bf16[128,4096]{1,0:T(8,128)(2,1)S(1)}, bf16[128,4096]{1,0:T(8,128)(2,1)}, u32[]{:S(2)}) copy-start(bf16[128,4096]{1,0:T(8,128)(2,1)} %param.9) | copy-start | bytes 3145732
  6.5 46.4 %all-gather.4.cloned.1.call-start = ((), (), s32[]{:S(2)}) async-start(), calls=%async_computation.1 | async-start | bytes 5898240 | tf_op jit(solution)/shard_map/all_gather | solution.py:96
  8.8 246.4 %all-gather.6.cloned.1.call-start = ((), (), s32[]{:S(2)}) async-start(), calls=%async_computation.2 | async-start | bytes 9437184 | tf_op jit(solution)/shard_map/all_gather | solution.py:119
  21.1 1.4 copy-start.1
  199.2 156.8 %reduce-scatter.2.cloned.1.call-start = ((), (), s32[]{:S(2)}) async-start(), calls=%async_computation.3 | async-start | bytes 5242880 | tf_op jit(solution)/shard_map/reduce_scatter | solution.py:123
Sparse Core Ops, SparseCore 0:
  9.2 43.6 all-gather.3
  199.4 55.8 all-gather.5
  279.2 76.7 reduce-scatter.1
where the time goes:
time: 364 us; the launch traced here: 363 us
  waiting for transfers between devices  155 us (43%)
  matrix products  84.4 us (23%)
  other arithmetic  45.1 us (12%)
  local copies, waits for them, and re-layouts  39.9 us (11%)
  blocking collectives  17.8 us (5%)
  between operations  13.8 us (4%)
  loops' own time  6.6 us (2%)
    reduce_scatter x1, waiting for transfers between devices, body(): lax.psum_scatter(terms.astype(jnp.bfloat16), 'tp', scatter_dimension=0, t...  77 us
    all_gather x1, waiting for transfers between devices, body(): lax.all_gather(attended, 'ctx', axis=0, tiled=True)  55.8 us
    dot_general x16, matrix products, absorb(): jnp.einsum('kgtn,nkd->kgtd', raised.astype(jnp.bfloat16), value_matrix, p...  40.5 us
    dot_general x1, matrix products, body(): jnp.dot(lax.all_gather(attended, 'ctx', axis=0, tiled=True), out_weight,...  23.8 us
    all_gather x1, waiting for transfers between devices, body(): piece = lax.all_gather(key_value_cache, 'ctx', axis=1, tiled=True)  22.1 us
    dot_general x16, matrix products, absorb(): jnp.einsum('tkgd,nkd->kgtn', query_heads, key_matrix, preferred_element_t...  20 us
    reduce_sum x16, other arithmetic, absorb(): new_total = running_total * rescale + jnp.sum(raised, axis=-1)  19.3 us
    dynamic_slice x8, local copies, waits for them, and re-layouts, one_shard(): lax.dynamic_slice_in_dim(piece, number_count * SHARD_ROWS, SHARD_ROWS, 1)  15.8 us
  transfers between devices with their start and end apart: 3, of which 3 were waited for; matrix products, arithmetic and copies ran while one was open for 1% of the time, Pallas kernels for 0%

commit v1 on v0

v1 whole, which is shorter than its diff:
```python
import functools
import math

import jax
import jax.numpy as jnp
from jax import lax
from jax.experimental import pallas as pl
from jax.experimental.pallas import tpu as pltpu
from jax.sharding import PartitionSpec as P

QUERY_HEADS = 128
KEY_VALUE_HEADS = 8
HEAD_SIZE = 128
CACHE_DEV = 512

GROUP = QUERY_HEADS // KEY_VALUE_HEADS
ROW_BLOCK = 128
BLOCKS_PER_STEP = 4
HEADS_PER_STEP = 4
NEVER = 2**30
masked_floor = -1e30


def attention_kernel(last_block, steps_ref, table_ref, query_ref, own_ref, order_ref, kv_ref, out_ref):
    tokens = query_ref.shape[0]
    heads = query_ref.shape[1] // HEAD_SIZE
    queries = jnp.concatenate(
        [query_ref[:, h * HEAD_SIZE : (h + 1) * HEAD_SIZE] for h in range(heads)], axis=0
    )
    factor = math.log2(math.e) / math.sqrt(HEAD_SIZE)
    own = jnp.concatenate([own_ref[...]] * heads, axis=1)

    def step(i, carry):
        peak, total, weighted = carry
        keys, values, orders = [], [], []
        for b in range(BLOCKS_PER_STEP):
            entry = table_ref[i * BLOCKS_PER_STEP + b]
            rows = pl.ds(pl.multiple_of(jnp.minimum(entry, last_block) * ROW_BLOCK, ROW_BLOCK), ROW_BLOCK)
            keys.append(kv_ref[0, rows, :])
            values.append(kv_ref[1, rows, :])
            marks = pl.ds(pl.multiple_of(entry * ROW_BLOCK, ROW_BLOCK), ROW_BLOCK)
            orders.append(order_ref[marks, :])
        scores = lax.dot_general(
            jnp.concatenate(keys, axis=0),
            queries,
            (((1,), (1,)), ((), ())),
            preferred_element_type=jnp.float32,
        )
        order = jnp.concatenate(orders, axis=0)
        order = jnp.concatenate([order] * (tokens * heads // order.shape[1]), axis=1)
        scores = jnp.where(order <= own, scores, -jnp.inf)
        new_peak = jnp.maximum(peak, jnp.max(scores, axis=0, keepdims=True))
        rescale = jnp.exp2((peak - new_peak) * factor)
        raised = jnp.exp2((scores - new_peak) * factor)
        total = total * rescale + jnp.sum(raised, axis=0, keepdims=True)
        update = lax.dot_general(
            jnp.concatenate(values, axis=0),
            raised.astype(jnp.bfloat16),
            (((0,), (0,)), ((), ())),
            preferred_element_type=jnp.float32,
        )
        return new_peak, total, weighted * rescale + update

    width = tokens * heads
    start = (
        jnp.full((1, width), masked_floor, jnp.float32),
        jnp.zeros((1, width), jnp.float32),
        jnp.zeros((HEAD_SIZE, width), jnp.float32),
    )
    _, total, weighted = lax.fori_loop(0, steps_ref[0], step, start)
    result = weighted / total
    for h in range(heads):
        out_ref[:, h * HEAD_SIZE : (h + 1) * HEAD_SIZE] = result[:, h * tokens : (h + 1) * tokens].T.astype(
            out_ref.dtype
        )


def attention(queries, kv_all, own_order, order_all, lengths_all):
    tokens, columns = queries.shape
    kv_rows = kv_all.shape[1]
    shards = lengths_all.shape[0]
    shard_rows = kv_rows // shards
    kv_heads = kv_all.shape[2] // HEAD_SIZE
    per_group = GROUP // HEADS_PER_STEP
    slot = jnp.arange(CACHE_DEV)
    cache_order = jnp.where(slot[None, :] < lengths_all[:, None], -1, NEVER)
    row_order = jnp.concatenate([cache_order, order_all.reshape(shards, -1)], axis=1).reshape(kv_rows)
    row_order = jnp.concatenate([row_order, jnp.full((ROW_BLOCK,), NEVER, jnp.int32)])
    row_order = jnp.broadcast_to(row_order[:, None], (kv_rows + ROW_BLOCK, 128)).astype(jnp.int32)
    blocks = kv_rows // ROW_BLOCK
    within = jnp.arange(shard_rows // ROW_BLOCK) * ROW_BLOCK
    wanted = ((within[None, :] >= CACHE_DEV) | (within[None, :] < lengths_all[:, None])).reshape(blocks)
    place = jnp.cumsum(wanted.astype(jnp.int32)) - 1
    slots = -(-blocks // BLOCKS_PER_STEP) * BLOCKS_PER_STEP
    hit = wanted[None, :] & (place[None, :] == jnp.arange(slots)[:, None])
    table = jnp.where(
        jnp.any(hit, axis=1), jnp.sum(jnp.where(hit, jnp.arange(blocks)[None, :], 0), axis=1), blocks
    ).astype(jnp.int32)
    count = jnp.sum(wanted.astype(jnp.int32))
    steps = ((count + BLOCKS_PER_STEP - 1) // BLOCKS_PER_STEP).reshape(1).astype(jnp.int32)
    query_block = HEADS_PER_STEP * HEAD_SIZE
    return pl.pallas_call(
        functools.partial(attention_kernel, blocks - 1),
        out_shape=jax.ShapeDtypeStruct((tokens, columns), jnp.bfloat16),
        grid_spec=pltpu.PrefetchScalarGridSpec(
            num_scalar_prefetch=2,
            grid=(kv_heads, per_group),
            in_specs=[
                pl.BlockSpec((tokens, query_block), lambda g, h, *_: (0, g * per_group + h)),
                pl.BlockSpec((1, tokens), lambda g, h, *_: (0, 0)),
                pl.BlockSpec((kv_rows + ROW_BLOCK, 128), lambda g, h, *_: (0, 0)),
                pl.BlockSpec((2, kv_rows, HEAD_SIZE), lambda g, h, *_: (0, 0, g)),
            ],
            out_specs=pl.BlockSpec((tokens, query_block), lambda g, h, *_: (0, g * per_group + h)),
        ),
        compiler_params=pltpu.CompilerParams(vmem_limit_bytes=40 * 1024 * 1024),
        cost_estimate=pl.CostEstimate(
            flops=4 * tokens * columns * kv_rows, bytes_accessed=8 * 2**20, transcendentals=tokens * kv_rows * 32
        ),
        name="attend",
    )(steps, table, queries, own_order[None, :], row_order, kv_all)


def gather_metadata(cache_lengths, token_order):
    tokens = token_order.shape[0]
    packed = lax.all_gather(jnp.concatenate([token_order, cache_lengths]), "ctx", axis=0, tiled=False)
    return packed[:, :tokens].reshape(-1), packed[:, tokens]


def body(queries, key_value_cache, cache_lengths, token_order, out_weight):
    order_all, lengths_all = gather_metadata(cache_lengths, token_order)
    kv_all = lax.all_gather(key_value_cache, "ctx", axis=1, tiled=True)
    attended = attention(queries, kv_all, token_order, order_all, lengths_all)
    terms = jnp.dot(
        lax.all_gather(attended, "ctx", axis=0, tiled=True),
        out_weight,
        preferred_element_type=jnp.float32,
    )
    return lax.psum_scatter(terms.astype(jnp.bfloat16), "tp", scatter_dimension=0, tiled=True)


def solution(mesh):
    placed = (P("ctx", "tp"), P(None, "ctx", "tp"), P("ctx"), P("ctx"), P("tp", "ctx"))
    return jax.shard_map(
        body, mesh=mesh, in_specs=placed, out_specs=P("tp", "ctx"), check_vma=False
    )
```

time: 364 us -> 256 us (0.70)
  matrix products: 84.4 us -> 23.7 us
  other arithmetic: 45.1 us -> 2 us
  Pallas kernels: 0 us -> 36.4 us
  local copies, waits for them, and re-layouts: 39.9 us -> 6.72 us
  blocking collectives: 17.8 us -> 9.62 us
  waiting for transfers between devices: 155 us -> 162 us
  loops' own time: 6.6 us -> 0 us
    dot_general x32 -> x0, matrix products: 60.6 us -> none  [the longest x16 40.5 us: absorb(): jnp.einsum('kgtn,nkd->kgtd', raised.astype(jnp.bfloat16), value_matrix, p...]
    pallas_call x0 -> x1, Pallas kernels: none -> 36.4 us  [attention(): pl.pallas_call(functools.partial(attention_kernel, blocks - 1), out_shape...]
    reduce_sum x24 -> x2, other arithmetic: 25 us -> 0.75 us  [the longest x1 0.64 us: attention(): count = jnp.sum(wanted.astype(jnp.int32))]
    dynamic_slice x17 -> x0, local copies, waits for them, and re-layouts: 16.5 us -> none  [the longest x8 15.8 us: one_shard(): lax.dynamic_slice_in_dim(piece, number_count * SHARD_ROWS, SHARD_ROWS, 1)]
    slice x16 -> x2, local copies, waits for them, and re-layouts: 15.7 us -> 0.12 us  [gather_metadata(): return (packed[:, :tokens].reshape(-1), packed[:, tokens])]
    while x16 -> x0, other arithmetic: 12.3 us -> none
    all_gather x1, waiting for transfers between devices: 22.1 us -> 30.4 us  [body(): kv_all = lax.all_gather(key_value_cache, 'ctx', axis=1, tiled=True)]
    all_gather x1 -> x0, blocking collectives: 8.27 us -> none  [body(): lax.all_gather(token_order, 'ctx', axis=0, tiled=True)]
where the time goes in v1:
time: 256 us
  waiting for transfers between devices  162 us (63%)
  Pallas kernels  36.4 us (14%)
  matrix products  23.7 us (9%)
  between operations  15.2 us (6%)
  blocking collectives  9.62 us (4%)
  local copies, waits for them, and re-layouts  6.72 us (3%)
    reduce_scatter x1, waiting for transfers between devices, body(): lax.psum_scatter(terms.astype(jnp.bfloat16), 'tp', scatter_dimension=0, t...  77 us
    all_gather x1, waiting for transfers between devices, body(): lax.all_gather(attended, 'ctx', axis=0, tiled=True)  54.4 us
    pallas_call x1, Pallas kernels, attention(): pl.pallas_call(functools.partial(attention_kernel, blocks - 1), out_shape...  36.4 us
    all_gather x1, waiting for transfers between devices, body(): kv_all = lax.all_gather(key_value_cache, 'ctx', axis=1, tiled=True)  30.4 us
    dot_general x1, matrix products, body(): jnp.dot(lax.all_gather(attended, 'ctx', axis=0, tiled=True), out_weight,...  23.7 us
    unnamed x1, blocking collectives  9.62 us
    unnamed x8, local copies, waits for them, and re-layouts  5.61 us
  transfers between devices with their start and end apart: 3, of which 3 were waited for; matrix products, arithmetic and copies ran while one was open for 1% of the time, Pallas kernels for 0%

profile of v1, /device:TPU:0, one launch (start us, length us, event | category | flops | bytes accessed | tf_op | source)
XLA Modules:
  0.0 256.1 jit_solution(14086234166621590667)
XLA Ops:
  6.5 0.7 all-gather.4.cloned.1.call-update
  7.9 1.2 dynamic-slice
  9.9 0.8 add_dynamic-update-slice_fusion
  10.6 9.6 %all-reduce.1 = s32[1032]{0:T(1024)S(1)} all-reduce(s32[1032]{0:T(1024)S(1)} %add_dynamic-update-slice_fusion), channel_id=2, replica_groups=mesh['ctx'=8,'tp'=4] {'ctx'}, use_global_device_ids=true, to_apply=%add.1 | all-reduce | flops 1032 | bytes 8256
  20.3 0.1 reshape.105
  20.4 0.1 slice_reduce_fusion
  20.5 0.1 fusion.3
  20.6 0.6 convert_reduce_fusion
  21.9 0.1 or.29
  21.9 0.1 fusion.2
  22.0 0.1 reshape.111
  22.1 0.1 reduce-window.8
  22.2 0.1 add_reduce_fusion
  22.3 0.1 fusion.1
  22.4 0.1 select_reduce_fusion
  22.6 30.4 %all-gather.4.cloned.1.call-done.kv_ref = bf16[2,5120,256]{2,1,0:T(8,128)(2,1)} async-done(((bf16[2,640,256]{2,1,0:T(8,128)(2,1)}), bf16[2,5120,256]{2,1,0:T(8,128)(2,1)}) %all-gather.4.cloned.1.call-update) | async-done | bytes 5242896 | tf_op jit(solution)/shard_map/all_gather | solution.py:132
  53.0 0.7 broadcast_in_dim.46.order_ref
  53.7 0.7 copy-done
  54.4 2.5 copy-done.1
  56.9 1.2 copy-done.2
  58.1 36.4 %attend.1 = bf16[128,4096]{1,0:T(8,128)(2,1)} custom-call(s32[1]{0:T(128)} %bitcast.1.steps_ref, s32[40]{0:T(128)S(1)} %broadcast_select_fusion.table_ref, bf16[128,4096]{1,0:T(8,128)(2,1)S(1)} %copy-done.2, s32[1,128]{1,0:T(1,128)S(1)} %bitcast.5, s32[5248,128]{1,0:T(8,128)S(1)} %broadcast_in_dim.46.order_ref, bf16[2,5120,256]{2,1,0:T(8,128)(2,1)S(1)} %copy-done.1), custom_call_target="tpu_custom_call" | custom-call | flops 10737418240 | bytes 8388608 | tf_op jit(solution)/shard_map/attend/pallas_call | solution.py:102
  94.6 54.4 %all-gather.6.cloned.1.call-done = bf16[1024,4096]{1,0:T(8,128)(2,1)} async-done(((bf16[128,4096]{1,0:T(8,128)(2,1)}), bf16[1024,4096]{1,0:T(8,128)(2,1)}) %all-gather.6.cloned.1.call-update) | async-done | bytes 8388624 | tf_op jit(solution)/shard_map/all_gather | solution.py:135
  148.9 23.7 %convolution_convert_fusion = bf16[1024,2048]{1,0:T(8,128)(2,1)} fusion(bf16[1024,4096]{1,0:T(8,128)(2,1)} %all-gather.6.cloned.1.call-done, bf16[4096,2048]{1,0:T(8,128)(2,1)} %param.9), kind=kOutput, calls=%fused_computation | convolution fusion | flops 17181966336 | bytes 29360128 | tf_op jit(solution)/shard_map/dot_general | solution.py:134
  172.6 77.0 %reduce-scatter.2.cloned.1.call-done = bf16[256,2048]{1,0:T(8,128)(2,1)} async-done(((bf16[1024,2048]{1,0:T(8,128)(2,1)}), bf16[256,2048]{1,0:T(8,128)(2,1)}) %reduce-scatter.2.cloned.1.call-update) | async-done | bytes 1048592 | tf_op jit(solution)/shard_map/reduce_scatter | solution.py:139
  (16 shorter events, 0.2 us)
Async XLA Ops:
  6.5 46.4 %all-gather.4.cloned.1.call-start = ((), (), s32[]{:S(2)}) async-start(), calls=%async_computation.1 | async-start | bytes 5898240 | tf_op jit(solution)/shard_map/all_gather | solution.py:132
  7.3 141.7 %all-gather.6.cloned.1.call-start = ((), (), s32[]{:S(2)}) async-start(), calls=%async_computation.2 | async-start | bytes 9437184 | tf_op jit(solution)/shard_map/all_gather | solution.py:135
  53.7 0.7 copy-start
  54.4 2.5 copy-start.1
  56.9 1.2 copy-start.2
  94.5 155.1 %reduce-scatter.2.cloned.1.call-start = ((), (), s32[]{:S(2)}) async-start(), calls=%async_computation.3 | async-start | bytes 5242880 | tf_op jit(solution)/shard_map/reduce_scatter | solution.py:139
Sparse Core Ops, SparseCore 0:
  9.2 43.6 all-gather.3
  94.6 54.2 all-gather.5
  172.8 76.7 reduce-scatter.1

commit v2 on v1

--- a/solution.py
+++ b/solution.py
@@ -16,7 +16,8 @@
 GROUP = QUERY_HEADS // KEY_VALUE_HEADS
 ROW_BLOCK = 128
 BLOCKS_PER_STEP = 4
-HEADS_PER_STEP = 4
+HEADS_PER_STEP = 8
+PIECES = 2
 NEVER = 2**30
 masked_floor = -1e30
 
@@ -28,7 +29,7 @@
         [query_ref[:, h * HEAD_SIZE : (h + 1) * HEAD_SIZE] for h in range(heads)], axis=0
     )
     factor = math.log2(math.e) / math.sqrt(HEAD_SIZE)
-    own = jnp.concatenate([own_ref[...]] * heads, axis=1)
+    own = own_ref[...]
 
     def step(i, carry):
         peak, total, weighted = carry
@@ -68,20 +69,15 @@
         jnp.zeros((HEAD_SIZE, width), jnp.float32),
     )
     _, total, weighted = lax.fori_loop(0, steps_ref[0], step, start)
-    result = weighted / total
+    result = (weighted / total).T
     for h in range(heads):
-        out_ref[:, h * HEAD_SIZE : (h + 1) * HEAD_SIZE] = result[:, h * tokens : (h + 1) * tokens].T.astype(
-            out_ref.dtype
-        )
+        out_ref[:, h * HEAD_SIZE : (h + 1) * HEAD_SIZE] = result[h * tokens : (h + 1) * tokens].astype(out_ref.dtype)
 
 
-def attention(queries, kv_all, own_order, order_all, lengths_all):
-    tokens, columns = queries.shape
+def attention_tables(kv_all, order_all, lengths_all):
     kv_rows = kv_all.shape[1]
     shards = lengths_all.shape[0]
     shard_rows = kv_rows // shards
-    kv_heads = kv_all.shape[2] // HEAD_SIZE
-    per_group = GROUP // HEADS_PER_STEP
     slot = jnp.arange(CACHE_DEV)
     cache_order = jnp.where(slot[None, :] < lengths_all[:, None], -1, NEVER)
     row_order = jnp.concatenate([cache_order, order_all.reshape(shards, -1)], axis=1).reshape(kv_rows)
@@ -98,6 +94,15 @@
     ).astype(jnp.int32)
     count = jnp.sum(wanted.astype(jnp.int32))
     steps = ((count + BLOCKS_PER_STEP - 1) // BLOCKS_PER_STEP).reshape(1).astype(jnp.int32)
+    return steps, table, row_order
+
+
+def attention(queries, kv_all, own_order, steps, table, row_order):
+    tokens, columns = queries.shape
+    kv_rows = kv_all.shape[1]
+    blocks = kv_rows // ROW_BLOCK
+    kv_heads = kv_all.shape[2] // HEAD_SIZE
+    per_group = GROUP // HEADS_PER_STEP
     query_block = HEADS_PER_STEP * HEAD_SIZE
     return pl.pallas_call(
         functools.partial(attention_kernel, blocks - 1),
@@ -107,7 +112,7 @@
             grid=(kv_heads, per_group),
             in_specs=[
                 pl.BlockSpec((tokens, query_block), lambda g, h, *_: (0, g * per_group + h)),
-                pl.BlockSpec((1, tokens), lambda g, h, *_: (0, 0)),
+                pl.BlockSpec((1, tokens * HEADS_PER_STEP), lambda g, h, *_: (0, 0)),
                 pl.BlockSpec((kv_rows + ROW_BLOCK, 128), lambda g, h, *_: (0, 0)),
                 pl.BlockSpec((2, kv_rows, HEAD_SIZE), lambda g, h, *_: (0, 0, g)),
             ],
@@ -118,7 +123,7 @@
             flops=4 * tokens * columns * kv_rows, bytes_accessed=8 * 2**20, transcendentals=tokens * kv_rows * 32
         ),
         name="attend",
-    )(steps, table, queries, own_order[None, :], row_order, kv_all)
+    )(steps, table, queries, jnp.tile(own_order, HEADS_PER_STEP)[None, :], row_order, kv_all)
 
 
 def gather_metadata(cache_lengths, token_order):
@@ -130,13 +135,21 @@
 def body(queries, key_value_cache, cache_lengths, token_order, out_weight):
     order_all, lengths_all = gather_metadata(cache_lengths, token_order)
     kv_all = lax.all_gather(key_value_cache, "ctx", axis=1, tiled=True)
-    attended = attention(queries, kv_all, token_order, order_all, lengths_all)
-    terms = jnp.dot(
-        lax.all_gather(attended, "ctx", axis=0, tiled=True),
-        out_weight,
-        preferred_element_type=jnp.float32,
-    )
-    return lax.psum_scatter(terms.astype(jnp.bfloat16), "tp", scatter_dimension=0, tiled=True)
+    tables = attention_tables(kv_all, order_all, lengths_all)
+    tokens = queries.shape[0]
+    piece = tokens // PIECES
+    parts = []
+    for number in range(PIECES):
+        own = slice(number * piece, (number + 1) * piece)
+        attended = attention(queries[own], kv_all, token_order[own], *tables)
+        terms = jnp.dot(
+            lax.all_gather(attended, "ctx", axis=0, tiled=True),
+            out_weight,
+            preferred_element_type=jnp.float32,
+        )
+        part = lax.psum_scatter(terms.astype(jnp.bfloat16), "tp", scatter_dimension=0, tiled=True)
+        parts.append(part.reshape(-1, piece, part.shape[1]))
+    return jnp.concatenate(parts, axis=1).reshape(-1, out_weight.shape[1])
 
 
 def solution(mesh):

time: 256 us -> 252 us (0.984)
  waiting for transfers between devices: 162 us -> 143 us
  matrix products: 23.7 us -> 29.1 us
  local copies, waits for them, and re-layouts: 6.72 us -> 11.4 us
    all_gather x1 -> x2, waiting for transfers between devices: 54.4 us -> 38.6 us  [body(): lax.all_gather(attended, 'ctx', axis=0, tiled=True)]
    dot_general x1 -> x2, matrix products: 23.7 us -> 29.1 us  [body(): jnp.dot(lax.all_gather(attended, 'ctx', axis=0, tiled=True), out_weight,...]
    all_gather x1, waiting for transfers between devices: 30.4 us -> 27.4 us  [body(): kv_all = lax.all_gather(key_value_cache, 'ctx', axis=1, tiled=True)]
    slice x0 -> x2, local copies, waits for them, and re-layouts: none -> 2.9 us  [body(): attended = attention(queries[own], kv_all, token_order[own], *tables)]
    pallas_call x1 -> x2, Pallas kernels: 36.4 us -> 38.6 us  [attention(): pl.pallas_call(functools.partial(attention_kernel, blocks - 1), out_shape...]
    reduce_scatter x1 -> x2, waiting for transfers between devices: 77 us -> 76.2 us  [body(): lax.psum_scatter(terms.astype(jnp.bfloat16), 'tp', scatter_dimension=0, t...]
  transfers between devices with their start and end apart: 3 -> 5, of which waited for: 3 -> 5; matrix products, arithmetic and copies ran while one was open for 1% -> 14% of each run, Pallas kernels for 0% -> 8%
where the time goes in v2:
time: 252 us; the launch traced here: 251 us
  waiting for transfers between devices  143 us (57%)
  Pallas kernels  38.6 us (15%)
  matrix products  29.1 us (12%)
  between operations  15.2 us (6%)
  local copies, waits for them, and re-layouts  11.4 us (5%)
  blocking collectives  9.62 us (4%)
  other arithmetic  4.27 us (2%)
    reduce_scatter x2, waiting for transfers between devices, body(): lax.psum_scatter(terms.astype(jnp.bfloat16), 'tp', scatter_dimension=0, t...  76.2 us
    all_gather x2, waiting for transfers between devices, body(): lax.all_gather(attended, 'ctx', axis=0, tiled=True)  38.6 us
    pallas_call x2, Pallas kernels, attention(): pl.pallas_call(functools.partial(attention_kernel, blocks - 1), out_shape...  38.6 us
    dot_general x2, matrix products, body(): jnp.dot(lax.all_gather(attended, 'ctx', axis=0, tiled=True), out_weight,...  29.1 us
    all_gather x1, waiting for transfers between devices, body(): kv_all = lax.all_gather(key_value_cache, 'ctx', axis=1, tiled=True)  27.4 us
    unnamed x1, blocking collectives  9.62 us
    unnamed x8, local copies, waits for them, and re-layouts  7.26 us
  transfers between devices with their start and end apart: 5, of which 5 were waited for; matrix products, arithmetic and copies ran while one was open for 14% of the time, Pallas kernels for 8%

profile of v2, /device:TPU:0, one launch (start us, length us, event | category | flops | bytes accessed | tf_op | source)
XLA Modules:
  0.0 251.4 jit_solution(10513719409113385743)
XLA Ops:
  6.5 0.7 all-gather.5.cloned.1.call-update
  7.9 1.2 dynamic-slice
  9.9 0.8 add_dynamic-update-slice_fusion
  10.6 9.6 %all-reduce.1 = s32[1032]{0:T(1024)S(1)} all-reduce(s32[1032]{0:T(1024)S(1)} %add_dynamic-update-slice_fusion), channel_id=2, replica_groups=mesh['ctx'=8,'tp'=4] {'ctx'}, use_global_device_ids=true, to_apply=%add.1 | all-reduce | flops 1032 | bytes 8256
  20.4 0.1 slice_reduce_fusion
  20.6 0.6 convert_reduce_fusion
  21.9 0.8 fusion.5
  23.2 0.1 fusion.1
  23.3 0.1 select_reduce_fusion
  23.4 2.1 fusion.4
  25.5 27.4 %all-gather.5.cloned.1.call-done.kv_ref = bf16[2,5120,256]{2,1,0:T(8,128)(2,1)} async-done(((bf16[2,640,256]{2,1,0:T(8,128)(2,1)}), bf16[2,5120,256]{2,1,0:T(8,128)(2,1)}) %all-gather.5.cloned.1.call-update) | async-done | bytes 5242896 | tf_op jit(solution)/shard_map/all_gather | solution.py:137
  53.0 0.7 broadcast_in_dim.42.order_ref
  53.7 1.0 copy-done
  54.8 2.5 copy-done.1
  57.3 19.3 %attend.2 = bf16[64,4096]{1,0:T(8,128)(2,1)} custom-call(s32[1]{0:T(128)} %bitcast.1.steps_ref, s32[40]{0:T(128)S(1)} %broadcast_select_fusion.table_ref, bf16[64,4096]{1,0:T(8,128)(2,1)S(1)} %copy-done, s32[1,512]{1,0:T(1,128)S(1)} %broadcast_in_dim_tile.6.own_ref, s32[5248,128]{1,0:T(8,128)S(1)} %broadcast_in_dim.42.order_ref, ...), custom_call_target="tpu_custom_call" | custom-call | flops 5368709120 | bytes 8388608 | tf_op jit(solution)/shard_map/attend/pallas_call | solution.py:107
  76.7 2.5 copy-done.2
  79.2 19.3 %attend.3 = bf16[64,4096]{1,0:T(8,128)(2,1)} custom-call(s32[1]{0:T(128)} %bitcast.1.steps_ref, s32[40]{0:T(128)S(1)} %broadcast_select_fusion.table_ref, bf16[64,4096]{1,0:T(8,128)(2,1)S(1)} %get-tuple-element.8.query_ref, s32[1,512]{1,0:T(1,128)S(1)} %broadcast_in_dim_tile.7.own_ref, s32[5248,128]{1,0:T(8,128)S(1)} %broadcast_in_dim.42.order_ref, ...), custom_call_target="tpu_custom_call" | custom-call | flops 5368709120 | bytes 8388608 | tf_op jit(solution)/shard_map/attend/pallas_call | solution.py:107
  98.5 14.8 %all-gather.7.cloned.1.call-done = bf16[512,4096]{1,0:T(8,128)(2,1)} async-done(((bf16[64,4096]{1,0:T(8,128)(2,1)}), bf16[512,4096]{1,0:T(8,128)(2,1)}) %all-gather.7.cloned.1.call-update) | async-done | bytes 4194320 | tf_op jit(solution)/shard_map/all_gather | solution.py:146
  113.3 14.6 %convolution_convert_fusion.1 = bf16[512,2048]{1,0:T(8,128)(2,1)} fusion(bf16[512,4096]{1,0:T(8,128)(2,1)} %all-gather.7.cloned.1.call-done, bf16[4096,2048]{1,0:T(8,128)(2,1)} %param.9), kind=kOutput, calls=%fused_computation.1 | convolution fusion | flops 8590983168 | bytes 23068672 | tf_op jit(solution)/shard_map/dot_general | solution.py:145
  127.9 23.9 %all-gather.9.cloned.1.call-done = bf16[512,4096]{1,0:T(8,128)(2,1)} async-done(((bf16[64,4096]{1,0:T(8,128)(2,1)}), bf16[512,4096]{1,0:T(8,128)(2,1)}) %all-gather.9.cloned.1.call-update) | async-done | bytes 4194320 | tf_op jit(solution)/shard_map/all_gather | solution.py:146
  151.8 14.6 %convolution_convert_fusion = bf16[512,2048]{1,0:T(8,128)(2,1)} fusion(bf16[512,4096]{1,0:T(8,128)(2,1)} %all-gather.9.cloned.1.call-done, bf16[4096,2048]{1,0:T(8,128)(2,1)} %param.9), kind=kOutput, calls=%fused_computation | convolution fusion | flops 8590983168 | bytes 23068672 | tf_op jit(solution)/shard_map/dot_general | solution.py:145
  166.4 31.2 %reduce-scatter.3.cloned.1.call-done = bf16[128,2048]{1,0:T(8,128)(2,1)} async-done(((bf16[512,2048]{1,0:T(8,128)(2,1)}), bf16[128,2048]{1,0:T(8,128)(2,1)}) %reduce-scatter.3.cloned.1.call-update) | async-done | bytes 524304 | tf_op jit(solution)/shard_map/reduce_scatter | solution.py:150
  197.6 45.0 %reduce-scatter.5.cloned.1.call-done = bf16[128,2048]{1,0:T(8,128)(2,1)} async-done(((bf16[512,2048]{1,0:T(8,128)(2,1)}), bf16[128,2048]{1,0:T(8,128)(2,1)}) %reduce-scatter.5.cloned.1.call-update) | async-done | bytes 524304 | tf_op jit(solution)/shard_map/reduce_scatter | solution.py:150
  242.6 2.3 pad_maximum_fusion
  (31 shorter events, 1.0 us)
Async XLA Ops:
  6.5 46.4 %all-gather.5.cloned.1.call-start = ((), (), s32[]{:S(2)}) async-start(), calls=%async_computation.2 | async-start | bytes 5898240 | tf_op jit(solution)/shard_map/all_gather | solution.py:137
  7.3 106.0 %all-gather.7.cloned.1.call-start = ((), (), s32[]{:S(2)}) async-start(), calls=%async_computation.3 | async-start | bytes 4718592 | tf_op jit(solution)/shard_map/all_gather | solution.py:146
  53.7 1.0 copy-start
  54.8 2.5 copy-start.1
  76.6 75.3 %all-gather.9.cloned.1.call-start = ((), (), s32[]{:S(2)}) async-start(), calls=%async_computation.5 | async-start | bytes 4718592 | tf_op jit(solution)/shard_map/all_gather | solution.py:146
  76.7 2.5 copy-start.2
  98.5 99.1 %reduce-scatter.3.cloned.1.call-start = ((), (), s32[]{:S(2)}) async-start(), calls=%async_computation.4 | async-start | bytes 2621440 | tf_op jit(solution)/shard_map/reduce_scatter | solution.py:150
  127.9 114.7 %reduce-scatter.5.cloned.1.call-start = ((), (), s32[]{:S(2)}) async-start(), calls=%async_computation.6 | async-start | bytes 2621440 | tf_op jit(solution)/shard_map/reduce_scatter | solution.py:150
Sparse Core Ops, SparseCore 0:
  9.2 43.6 all-gather.4
  76.7 36.5 all-gather.6
  115.2 36.5 all-gather.8
  154.0 43.6 reduce-scatter.2
  199.8 42.8 reduce-scatter.4
